TPU v7x, 32 devices: a whole 2x2x4 slice. The times are simulated.
32 devices in a mesh: groups: 2 (over y), expert: 8 (over z, x), tensor: 2 (over core).
Axes of the slice: x: 2, y: 2, z: 4, core: 2. Of those that a mesh axis runs over, the one named last changes fastest.
Arguments:
- tokens: bfloat16 [4096, 1440], P(('groups', 'expert')), parts along dimension 0, may hold values from -6 to 6
- routes: int32 [4096, 4], P(('groups', 'expert')), parts along dimension 0, may hold values from 0 to 7, all different within a row; in each aligned block of 256 rows (0 to 255, 256 to 511, ...) at most 192 rows name the same one
- gates: float32 [4096, 4], P(('groups', 'expert')), parts along dimension 0, may hold values from 0.1 to 1
- w_gate: bfloat16 [8, 1440, 1440], P('expert', None, 'tensor'), may hold values from -0.15625 to 0.15625
- w_up: bfloat16 [8, 1440, 1440], P('expert', None, 'tensor'), may hold values from -0.15625 to 0.15625
- w_down: bfloat16 [8, 1440, 1440], P('expert', 'tensor'), may hold values from -0.15625 to 0.15625
- shared_gate: bfloat16 [1440, 1440], P(None, 'tensor'), may hold values from -0.15625 to 0.15625
- shared_up: bfloat16 [1440, 1440], P(None, 'tensor'), may hold values from -0.15625 to 0.15625
- shared_down: bfloat16 [1440, 1440], P('tensor'), may hold values from -0.15625 to 0.15625
Outputs:
- mixed: bfloat16 [4096, 1440], P(('groups', 'expert'), 'tensor'), parts along dimension 0
There are 2 independent parts, one for each index of `groups`. A program takes and returns all parts, laid end to end along the dimension named above; an argument that names none is the same for every part. Nothing has to cross between parts.
Inputs may be any that keep to these rules, and one draw needn't show every extreme that they name: `routes`: each token names 4 different experts. Among the 256 tokens of one index of expert (aligned blocks of rows), no expert is named by more than 192 tokens; in some blocks one expert is named by exactly 192.
All inputs are finite; a program needn't handle non-finite values.
Results may differ from a plain program's by a relative error of at most 0.0051.
Values may be sent and summed in bfloat16 or wider, within the bound.
A program may use at most 192 MiB of HBM per device.

v0:
```python
import functools

import jax
import jax.numpy as jnp
from jax import lax
from jax.experimental import pallas as pl
from jax.experimental.pallas import tpu as pltpu
from jax.sharding import PartitionSpec as P

MESH = pl.DeviceIdType.MESH
VMEM_BUDGET = 52 * 1024 * 1024


def exchange_local(tokens, routes, gates, w_gate, w_up, w_down, shared_gate, shared_up, shared_down):
    tok_count, top_count = routes.shape
    width_all = tokens.shape[1]
    local_experts = w_gate.shape[0]
    expert_count = lax.axis_size("expert")
    experts_all = expert_count * local_experts
    capacity = max(2, (3 * tok_count * top_count + 2 * experts_all - 1) // (2 * experts_all))
    flat_routes = routes.reshape(-1)
    onehot = (flat_routes[:, None] == jnp.arange(experts_all, dtype=jnp.int32)[None, :]).astype(
        jnp.int32
    )
    order_in = jnp.sum(jnp.cumsum(onehot, axis=0) * onehot, axis=1) - 1
    slot_index = flat_routes * capacity + order_in
    half_width = width_all // lax.axis_size("tensor")
    own_cols = lax.dynamic_slice_in_dim(
        tokens, lax.axis_index("tensor") * half_width, half_width, 1
    )
    outgoing = jnp.zeros((experts_all * capacity, half_width), jnp.bfloat16)
    outgoing = outgoing.at[slot_index].set(jnp.repeat(own_cols, top_count, axis=0))
    outgoing = outgoing.reshape(experts_all, capacity, half_width)
    received = lax.all_to_all(outgoing, "expert", split_axis=0, concat_axis=0, tiled=True)
    received = lax.all_gather(received, "tensor", axis=2, tiled=True)
    item_rows = received.shape[1]
    stacked = received.reshape(expert_count, local_experts, item_rows, width_all)
    stacked = stacked.transpose(1, 0, 2, 3).reshape(
        local_experts, expert_count * item_rows, width_all
    )
    gate_val = jnp.einsum("emd,edf->emf", stacked, w_gate, preferred_element_type=jnp.float32)
    up_val = jnp.einsum("emd,edf->emf", stacked, w_up, preferred_element_type=jnp.float32)
    hidden = (jax.nn.silu(gate_val) * up_val).astype(jnp.bfloat16)
    partial_value = jnp.einsum("emf,efd->emd", hidden, w_down, preferred_element_type=jnp.float32)
    partial_value = partial_value.reshape(local_experts, expert_count, item_rows, width_all)
    partial_value = partial_value.transpose(1, 0, 2, 3).reshape(experts_all, item_rows, width_all)
    summed = lax.psum_scatter(partial_value, "tensor", scatter_dimension=2, tiled=True).astype(
        jnp.bfloat16
    )
    returned = lax.all_to_all(summed, "expert", split_axis=0, concat_axis=0, tiled=True)
    shared_g = jnp.dot(tokens, shared_gate, preferred_element_type=jnp.float32)
    shared_u = jnp.dot(tokens, shared_up, preferred_element_type=jnp.float32)
    shared_hidden = (jax.nn.silu(shared_g) * shared_u).astype(jnp.bfloat16)
    shared_part = jnp.dot(shared_hidden, shared_down, preferred_element_type=jnp.float32)
    picked = returned.reshape(experts_all * capacity, half_width)[slot_index]
    picked = picked.astype(jnp.float32).reshape(tok_count, top_count, half_width)
    routed = jnp.sum(gates[:, :, None] * picked, axis=1)
    total = routed + lax.psum_scatter(shared_part, "tensor", scatter_dimension=1, tiled=True)
    return (own_cols.astype(jnp.float32) + total).astype(jnp.bfloat16)


def silu_mul(g, u):
    return (g / (1.0 + jnp.exp(-g)) * u).astype(jnp.bfloat16)


def moe_kernel(nz, nx, width, tok_ref, routes_ref, gates_ref, wg_ref, wu_ref, wd_ref, sg_ref, su_ref, sd_ref, out_ref,
               X, Wg, Wu, Wd, Sg, Su, Sd, OWN, O, PXs, PXr, CSs, CSr, SHo, SHs, SHr, FXs, FXr,
               w_loc, s_loc, w_send, w_recv, z_send, z_recv, x_send, x_recv, p_send, p_recv,
               c_send, c_recv, m_send, m_recv):
    me = lax.axis_index("expert")
    core = lax.axis_index("tensor")
    z = me // nx
    x = me % nx
    ox = nx - 1 - x
    other = z * nx + ox
    rows = tok_ref.shape[0] // 2
    half = out_ref.shape[1]

    barrier = pltpu.get_barrier_semaphore()
    for d in range(1, nz):
        peer = ((z + d) % nz) * nx + x
        pl.semaphore_signal(barrier, inc=1, device_id={"expert": peer}, device_id_type=MESH)
    pl.semaphore_signal(barrier, inc=1, device_id={"expert": other}, device_id_type=MESH)
    pl.semaphore_signal(barrier, inc=1, device_id={"tensor": 1 - core}, device_id_type=MESH)

    loc_s = [pltpu.make_async_copy(a, b, s_loc.at[i]) for i, (a, b) in enumerate(
        ((sg_ref, Sg), (su_ref, Su), (sd_ref, Sd)))]
    loc_w = [pltpu.make_async_copy(a.at[0], b.at[0], w_loc.at[i]) for i, (a, b) in enumerate(
        ((wg_ref, Wg), (wu_ref, Wu), (wd_ref, Wd)))]
    for cp in loc_s + loc_w:
        cp.start()
    n_all = nz * nx
    lo = width // 128 * 128
    spare = X.shape[2] - lo

    def own_half(ref):
        return jnp.where(core == 0, ref[:, :rows], ref[:, rows:])
    named, gate = own_half(routes_ref), own_half(gates_ref)
    slot = lax.broadcasted_iota(jnp.int32, (spare, rows), 0) - (width - lo)
    dense = jnp.zeros((spare, rows), jnp.float32)
    for k in range(named.shape[0]):
        for term in range(3):
            dense = jnp.where(slot - term * n_all == named[k:k + 1, :], gate[k:k + 1, :], dense)
    hi = dense.astype(jnp.bfloat16).astype(jnp.float32)
    mid = (dense - hi).astype(jnp.bfloat16).astype(jnp.float32)
    low = dense - hi - mid
    terms = jnp.where(slot < n_all, hi, jnp.where(slot < 2 * n_all, mid, low))
    X[me, :, lo:] = terms.T.astype(jnp.bfloat16)
    X[me, :, :width] = tok_ref[pl.ds(pl.multiple_of(core * rows, rows), rows), :]
    pl.semaphore_wait(barrier, nz + 1)

    def remote(src, dst, ssem, rsem, **dev):
        return pltpu.make_async_remote_copy(src_ref=src, dst_ref=dst, send_sem=ssem, recv_sem=rsem,
                                            device_id=dev, device_id_type=MESH)

    def z_copy(zo, side):
        e = zo * nx + x
        peer = me + nx if side == 0 else me - nx
        return remote(X.at[e], X.at[e], z_send.at[side, zo], z_recv.at[zo], expert=peer)

    def x_copy(zo, col):
        e = zo * nx + col
        return remote(X.at[e], X.at[e], x_send.at[zo], x_recv.at[zo], expert=other)

    def forward_z(zo):
        @pl.when(jnp.logical_and(zo <= z, z + 1 < nz))
        def _():
            z_copy(zo, 0).start()

        @pl.when(jnp.logical_and(zo >= z, z >= 1))
        def _():
            z_copy(zo, 1).start()

    def forward_x(zo):
        x_copy(zo, x).start()

    def take_z(zo):
        z_copy(zo, 0).wait_recv()
        forward_z(zo)

    part = rows // 2

    def p_copy(zo, h):
        r = pl.ds(h * part, part)
        return remote(PXs.at[zo, r], PXr.at[zo, r], p_send.at[h, zo], p_recv.at[h, zo], expert=other)

    def c_copy(zo, slot, h):
        r = pl.ds(h * part, part)
        return remote(CSs.at[zo, r], CSr.at[slot, r], c_send.at[h, zo], c_recv.at[h, slot], expert=zo * nx + x)

    forward_z(z)
    forward_x(z)
    rem_w = [remote(a.at[0], b.at[1], w_send.at[i], w_recv.at[i], tensor=1 - core) for i, (a, b) in enumerate(
        ((wg_ref, Wg), (wu_ref, Wu), (wd_ref, Wd)))]
    for cp in rem_w:
        cp.start()

    table = [sorted(range(nz), key=lambda q: (abs(q - k), abs(2 * q + 1 - nz))) for k in range(nz)]

    def nth(i):
        r = table[0][i]
        for k in range(1, nz):
            r = jnp.where(z == k, table[k][i], r)
        return r

    for cp in loc_s:
        cp.wait()
    tok = tok_ref[...]
    sh = silu_mul(jnp.dot(tok, Sg[...], preferred_element_type=jnp.float32),
                  jnp.dot(tok, Su[...], preferred_element_type=jnp.float32))
    SHo[...] = jnp.dot(sh, Sd[...], preferred_element_type=jnp.float32)

    @pl.when(core == 0)
    def _():
        SHs[...] = SHo[:, half:]

    @pl.when(core == 1)
    def _():
        SHs[...] = SHo[:, :half]
    sh_copy = remote(SHs, SHr, m_send.at[0], m_recv.at[0], tensor=1 - core)
    sh_copy.start()

    for cp in loc_w:
        cp.wait()
    for cp in rem_w:
        cp.wait_recv()

    def compute(zo):
        base = zo * nx
        xs = X[pl.ds(base, nx)].reshape(nx * rows, X.shape[2])
        xin = xs[:, :width]
        O[...] = jnp.zeros_like(O)
        for hh in range(2):
            hid = silu_mul(jnp.dot(xin, Wg[hh], preferred_element_type=jnp.float32),
                           jnp.dot(xin, Wu[hh], preferred_element_type=jnp.float32))
            O[...] += jnp.dot(hid, Wd[hh], preferred_element_type=jnp.float32)
        tail = xs[:, lo:].astype(jnp.float32)
        lane = lax.broadcasted_iota(jnp.int32, tail.shape, 1) - (width - lo)
        hit = (lane == me) | (lane == me + n_all) | (lane == me + 2 * n_all)
        weight = jnp.sum(jnp.where(hit, tail, 0.0), axis=1, keepdims=True)
        O[...] = weight * O[...].astype(jnp.bfloat16).astype(jnp.float32)
        OWN[zo] = O[pl.ds(pl.multiple_of(x * rows, rows), rows), :]
        PXs[zo] = O[pl.ds(pl.multiple_of(ox * rows, rows), rows), :].astype(jnp.bfloat16)

    def column_sum(zo):
        for h in range(2):
            r = slice(h * part, (h + 1) * part)
            p_copy(zo, h).wait_recv()
            CSs[zo, r] = (OWN[zo, r] + PXr[zo, r].astype(jnp.float32)).astype(jnp.bfloat16)
            c_copy(zo, z, h).start()

    for i in range(nz):
        zi = nth(i)

        @pl.when(jnp.logical_or(z == 0, z == nz - 1))
        def _():
            if i + 1 < nz:
                take_z(nth(i + 1))
                forward_x(nth(i + 1))

        @pl.when(jnp.logical_and(z > 0, z < nz - 1))
        def _():
            if i == 0:
                for j in range(1, min(3, nz)):
                    take_z(nth(j))
                    forward_x(nth(j))
            else:
                if i + 2 < nz:
                    take_z(nth(i + 2))
                if 2 <= i < nz - 1:
                    forward_x(nth(i + 1))
        if i >= 3:
            column_sum(nth(i - 2))
        x_copy(zi, ox).wait_recv()
        compute(zi)
        if i > 0:
            for h in range(2):
                p_copy(zi, h).start()
    for h in range(2):
        p_copy(z, h).start()
    for i in range(max(1, nz - 2), nz):
        column_sum(nth(i))
    for h in range(2):
        p_copy(z, h).wait_recv()
    OWN[z] += PXr[z].astype(jnp.float32)
    for i in range(1, nz):
        zi = nth(i)
        for h in range(2):
            c_copy(zi, zi, h).wait_recv()
        OWN[z] += CSr[zi].astype(jnp.float32)

    @pl.when(core == 0)
    def _():
        FXs[...] = OWN[z, :, half:]

    @pl.when(core == 1)
    def _():
        FXs[...] = OWN[z, :, :half]
    fx_copy = remote(FXs, FXr, m_send.at[1], m_recv.at[1], tensor=1 - core)
    fx_copy.start()
    sh_copy.wait_recv()
    fx_copy.wait_recv()

    for cc in range(2):
        @pl.when(core == cc)
        def _():
            cols = slice(cc * half, (cc + 1) * half)
            for hh in range(2):
                rr = slice(hh * rows, (hh + 1) * rows)
                routed = OWN[z, :, cols] if hh == cc else FXr[...]
                total = tok_ref[rr, cols].astype(jnp.float32) + routed + (SHo[rr, cols] + SHr[rr, :])
                out_ref[rr, :] = total.astype(jnp.bfloat16)

    for cp in rem_w:
        cp.wait_send()
    sh_copy.wait_send()
    fx_copy.wait_send()
    for i in range(nz):
        zo = i

        @pl.when(jnp.logical_and(zo <= z, z + 1 < nz))
        def _():
            z_copy(zo, 0).wait_send()

        @pl.when(jnp.logical_and(zo >= z, z >= 1))
        def _():
            z_copy(zo, 1).wait_send()

        x_copy(zo, x).wait_send()
        for h in range(2):
            p_copy(zo, h).wait_send()

        @pl.when(zo != z)
        def _():
            for h in range(2):
                c_copy(zo, z, h).wait_send()


def pad(n, m):
    return -(-n // m) * m


def gather_plan(tok_count, width, expert_count, local_experts, hidden):
    if local_experts != 1 or expert_count % 2 or tok_count % 32 or width % 2:
        return None
    nz, rows = expert_count // 2, tok_count // 2
    ext = pad(width + 3 * expert_count, 128)
    if ext - width // 128 * 128 > 128:
        return None
    wide, hid, half = pad(width, 128), pad(hidden, 128), pad(width // 2, 128)
    weights = 9 * (2 * width * hid + pad(hidden, 16) * wide) * 2 // 3 + 0
    moved = expert_count * rows * ext * 2 + 4 * nz * rows * wide * 2 + nz * rows * wide * 4
    flat = tok_count * (2 * wide * 4 + 2 * half * 4 + 2 * wide * 2) + 2 * rows * half * 4
    return weights + moved + flat


def gather_local(tokens, routes, gates, w_gate, w_up, w_down, shared_gate, shared_up, shared_down):
    tok_count, width = tokens.shape
    hidden = w_gate.shape[2]
    n = lax.axis_size("expert")
    nx, nz = 2, n // 2
    rows, half = tok_count // 2, width // 2
    ext_w = pad(width + 3 * n, 128)
    bf, f32 = jnp.bfloat16, jnp.float32
    vm, dma = pltpu.VMEM, pltpu.SemaphoreType.DMA
    scratch = [
        vm((n, rows, ext_w), bf),
        vm((2, width, hidden), bf), vm((2, width, hidden), bf), vm((2, hidden, width), bf),
        vm((width, hidden), bf), vm((width, hidden), bf), vm((hidden, width), bf),
        vm((nz, rows, width), f32), vm((nx * rows, width), f32),
        vm((nz, rows, width), bf), vm((nz, rows, width), bf), vm((nz, rows, width), bf), vm((nz, rows, width), bf),
        vm((tok_count, width), f32), vm((tok_count, half), f32), vm((tok_count, half), f32),
        vm((rows, half), f32), vm((rows, half), f32),
        dma((3,)), dma((3,)), dma((3,)), dma((3,)), dma((2, nz)), dma((nz,)), dma((nz,)), dma((nz,)),
        dma((2, nz)), dma((2, nz)), dma((2, nz)), dma((2, nz)), dma((2,)), dma((2,)),
    ]
    in_vmem, in_hbm = pl.BlockSpec(memory_space=pltpu.VMEM), pl.BlockSpec(memory_space=pl.ANY)
    return pl.pallas_call(
        functools.partial(moe_kernel, nz, nx, width),
        out_shape=jax.ShapeDtypeStruct((tok_count, half), bf),
        in_specs=[in_vmem] * 3 + [in_hbm] * 6,
        out_specs=in_vmem,
        scratch_shapes=scratch,
        compiler_params=pltpu.CompilerParams(collective_id=0, has_side_effects=True, vmem_limit_bytes=60 * 1024 * 1024),
    )(tokens, routes.T, gates.T, w_gate, w_up, w_down, shared_gate, shared_up, shared_down)


def local(tokens, routes, gates, w_gate, *rest):
    need = gather_plan(*tokens.shape, lax.axis_size("expert"), w_gate.shape[0], w_gate.shape[2])
    if need is not None and lax.axis_size("tensor") == 2 and need <= VMEM_BUDGET:
        return gather_local(tokens, routes, gates, w_gate, *rest)
    return exchange_local(tokens, routes, gates, w_gate, *rest)


def solution(mesh):
    in_specs = (
        P(("groups", "expert"), None),
        P(("groups", "expert"), None),
        P(("groups", "expert"), None),
        P("expert", None, "tensor"),
        P("expert", None, "tensor"),
        P("expert", "tensor", None),
        P(None, "tensor"),
        P(None, "tensor"),
        P("tensor", None),
    )
    out_specs = P(("groups", "expert"), "tensor")
    return jax.shard_map(local, mesh=mesh, in_specs=in_specs, out_specs=out_specs, check_vma=False)
```

profile of v0, /device:TPU:1, one launch (start us, length us, event | category | flops | bytes accessed | tf_op | source)
XLA Modules:
  0.0 93.4 jit_solution(2385855431023868433)
XLA Ops:
  0.0 2.3 %copy.10.tok_ref = bf16[256,1440]{1,0:T(8,128)(2,1)} copy(bf16[256,1440]{0,1:T(8,128)(2,1)} %param.9) | data formatting | bytes 1474560 | tf_op args[0]
  2.3 89.3 %shard_map.91 = bf16[256,720]{1,0:T(8,128)(2,1)} custom-call(bf16[256,1440]{1,0:T(8,128)(2,1)} %copy.10.tok_ref, s32[4,256]{1,0:T(4,128)} %bitcast.2, f32[4,256]{1,0:T(4,128)} %bitcast.3, bf16[1,1440,720]{2,1,0:T(8,128)(2,1)} %wg_ref.1, bf16[1,1440,720]{2,1,0:T(8,128)(2,1)} %wu_ref.1, bf16[1,720,1440]{2,1,0:T(8,128)(2,1)} %wd_ref.1, ...), custom_call_target="tpu_custom_call" | custom-call | tf_op jit(solution)/shard_map/pallas_call | solution.py:338
  91.5 1.9 %copy.11 = bf16[256,720]{0,1:T(8,128)(2,1)} copy(bf16[256,720]{1,0:T(8,128)(2,1)} %shard_map.91) | data formatting | bytes 737280 | tf_op jit(solution)/shard_map/pallas_call | solution.py:338
where the time goes:
time: 93.7 us; the launch traced here: 93.4 us
  Pallas kernels  89.3 us (95%)
  local copies, waits for them, and re-layouts  4.17 us (4%)
    pallas_call x1, Pallas kernels, gather_local(): pl.pallas_call(functools.partial(moe_kernel, nz, nx, width), out_shape=ja...  89.3 us
    unnamed x1, local copies, waits for them, and re-layouts  2.27 us
    pallas_call x1, local copies, waits for them, and re-layouts, gather_local(): pl.pallas_call(functools.partial(moe_kernel, nz, nx, width), out_shape=ja...  1.91 us

commit v1 on v0

v1 whole, which is shorter than its diff:
```python
import functools

import jax
import jax.numpy as jnp
from jax import lax
from jax.experimental import pallas as pl
from jax.experimental.pallas import tpu as pltpu
from jax.sharding import PartitionSpec as P

MESH = pl.DeviceIdType.MESH
VMEM_BUDGET = 52 * 1024 * 1024


def exchange_local(tokens, routes, gates, w_gate, w_up, w_down, shared_gate, shared_up, shared_down):
    tok_count, top_count = routes.shape
    width_all = tokens.shape[1]
    local_experts = w_gate.shape[0]
    expert_count = lax.axis_size("expert")
    experts_all = expert_count * local_experts
    capacity = max(2, (3 * tok_count * top_count + 2 * experts_all - 1) // (2 * experts_all))
    flat_routes = routes.reshape(-1)
    onehot = (flat_routes[:, None] == jnp.arange(experts_all, dtype=jnp.int32)[None, :]).astype(
        jnp.int32
    )
    order_in = jnp.sum(jnp.cumsum(onehot, axis=0) * onehot, axis=1) - 1
    slot_index = flat_routes * capacity + order_in
    half_width = width_all // lax.axis_size("tensor")
    own_cols = lax.dynamic_slice_in_dim(
        tokens, lax.axis_index("tensor") * half_width, half_width, 1
    )
    outgoing = jnp.zeros((experts_all * capacity, half_width), jnp.bfloat16)
    outgoing = outgoing.at[slot_index].set(jnp.repeat(own_cols, top_count, axis=0))
    outgoing = outgoing.reshape(experts_all, capacity, half_width)
    received = lax.all_to_all(outgoing, "expert", split_axis=0, concat_axis=0, tiled=True)
    received = lax.all_gather(received, "tensor", axis=2, tiled=True)
    item_rows = received.shape[1]
    stacked = received.reshape(expert_count, local_experts, item_rows, width_all)
    stacked = stacked.transpose(1, 0, 2, 3).reshape(
        local_experts, expert_count * item_rows, width_all
    )
    gate_val = jnp.einsum("emd,edf->emf", stacked, w_gate, preferred_element_type=jnp.float32)
    up_val = jnp.einsum("emd,edf->emf", stacked, w_up, preferred_element_type=jnp.float32)
    hidden = (jax.nn.silu(gate_val) * up_val).astype(jnp.bfloat16)
    partial_value = jnp.einsum("emf,efd->emd", hidden, w_down, preferred_element_type=jnp.float32)
    partial_value = partial_value.reshape(local_experts, expert_count, item_rows, width_all)
    partial_value = partial_value.transpose(1, 0, 2, 3).reshape(experts_all, item_rows, width_all)
    summed = lax.psum_scatter(partial_value, "tensor", scatter_dimension=2, tiled=True).astype(
        jnp.bfloat16
    )
    returned = lax.all_to_all(summed, "expert", split_axis=0, concat_axis=0, tiled=True)
    shared_g = jnp.dot(tokens, shared_gate, preferred_element_type=jnp.float32)
    shared_u = jnp.dot(tokens, shared_up, preferred_element_type=jnp.float32)
    shared_hidden = (jax.nn.silu(shared_g) * shared_u).astype(jnp.bfloat16)
    shared_part = jnp.dot(shared_hidden, shared_down, preferred_element_type=jnp.float32)
    picked = returned.reshape(experts_all * capacity, half_width)[slot_index]
    picked = picked.astype(jnp.float32).reshape(tok_count, top_count, half_width)
    routed = jnp.sum(gates[:, :, None] * picked, axis=1)
    total = routed + lax.psum_scatter(shared_part, "tensor", scatter_dimension=1, tiled=True)
    return (own_cols.astype(jnp.float32) + total).astype(jnp.bfloat16)


def silu_mul(g, u):
    return (g / (1.0 + jnp.exp(-g)) * u).astype(jnp.bfloat16)


def moe_kernel(nz, nx, cap, tok_ref, routes_ref, gates_ref, wg_ref, wu_ref, wd_ref, sg_ref, su_ref, sd_ref, out_ref,
               TOK, X, XC, XO, XIN, YS, YC, CSs, CSr, OWN, O, SHB, SHr, MT, POS, WT, PCOL, U, Wg, Wu, Wd, Sg, Su, Sd,
               t_loc, w_loc, s_loc, w_send, w_recv, m_send, m_recv, z_send, z_recv, x_send, x_recv, d_send, d_recv,
               y_send, y_recv, e_send, e_recv, c_send, c_recv, h_send, h_recv):
    bf, f32 = jnp.bfloat16, jnp.float32
    me = lax.axis_index("expert")
    core = lax.axis_index("tensor")
    z = me // nx
    x = me % nx
    ox = nx - 1 - x
    other = z * nx + ox
    n = nz * nx
    rows = X.shape[1]
    half = out_ref.shape[1]
    ch = cap // 2
    top = routes_ref.shape[0]
    chunks = z_recv.shape[1]
    part = rows // chunks

    barrier = pltpu.get_barrier_semaphore()
    for d in range(1, n):
        pl.semaphore_signal(barrier, inc=1, device_id={"expert": (me + d) % n}, device_id_type=MESH)
    pl.semaphore_signal(barrier, inc=1, device_id={"tensor": 1 - core}, device_id_type=MESH)
    pl.semaphore_signal(barrier, inc=1, device_id={"expert": other, "tensor": 1 - core}, device_id_type=MESH)

    tok_in = pltpu.make_async_copy(tok_ref, TOK, t_loc)
    tok_in.start()
    loc_s = [pltpu.make_async_copy(a, b, s_loc.at[i]) for i, (a, b) in enumerate(
        ((sg_ref, Sg), (su_ref, Su), (sd_ref, Sd)))]
    loc_w = [pltpu.make_async_copy(a.at[0], b.at[0], w_loc.at[i]) for i, (a, b) in enumerate(
        ((wg_ref, Wg), (wu_ref, Wu), (wd_ref, Wd)))]
    for cp in loc_s + loc_w:
        cp.start()

    def remote(src, dst, ssem, rsem, **dev):
        return pltpu.make_async_remote_copy(src_ref=src, dst_ref=dst, send_sem=ssem, recv_sem=rsem,
                                            device_id=dev, device_id_type=MESH)

    MT[me, :top] = routes_ref[...].astype(f32)
    MT[me, top:] = gates_ref[...]
    U[...] = jnp.where(lax.broadcasted_iota(jnp.int32, U.shape, 0) < lax.broadcasted_iota(jnp.int32, U.shape, 1),
                       1.0, 0.0).astype(bf)

    def ranks(named, gate):
        mine, theirs = named == me.astype(f32), named == other.astype(f32)
        on = jnp.concatenate([jnp.sum(jnp.where(mine, 1.0, 0.0), axis=1),
                              jnp.sum(jnp.where(theirs, 1.0, 0.0), axis=1)], axis=0)
        place = jnp.dot(on.astype(bf), U[...], preferred_element_type=f32)
        return jnp.where(on > 0, place, -1.0), jnp.sum(jnp.where(mine, gate, 0.0), axis=1)

    place, _ = ranks(routes_ref[...].astype(f32)[None], gates_ref[...][None])
    POS[pl.ds(me, 1), :] = place[:1]
    POS[pl.ds(n + me, 1), :] = place[1:]
    tok_in.wait()
    for cc in range(2):
        @pl.when(core == cc)
        def _():
            X[z] = TOK[:, cc * half:(cc + 1) * half]
    pl.semaphore_wait(barrier, n + 1)

    def m_copy(e, d):
        return remote(MT.at[e], MT.at[e], m_send.at[d], m_recv.at[e], expert=(me + d) % n)

    def z_copy(zo, side, k):
        r = pl.ds(k * part, part)
        return remote(X.at[zo, r], X.at[zo, r], z_send.at[side, zo, k], z_recv.at[zo, k],
                      expert=me + nx if side == 0 else me - nx)

    def x_copy(zo, k, source):
        return remote(XC.at[zo, pl.ds(k * ch, ch)], XIN.at[zo, source, pl.ds(ch, ch)], x_send.at[k, zo],
                      x_recv.at[source, zo], expert=other, tensor=k)

    def d_copy(zo, source):
        return remote(XO.at[zo], XIN.at[zo, source, pl.ds(0, ch)], d_send.at[zo], d_recv.at[zo], tensor=1 - core)

    def y_copy(zo, k, source):
        r = pl.ds(pl.multiple_of(cap + source * ch, ch), ch)
        return remote(YS.at[zo, k, pl.ds(ch, ch)], YC.at[zo, r], y_send.at[k, zo], y_recv.at[source, zo],
                      expert=other, tensor=k)

    def e_copy(zo, source):
        r = pl.ds(pl.multiple_of(source * ch, ch), ch)
        return remote(YS.at[zo, 1 - core, pl.ds(0, ch)], YC.at[zo, r], e_send.at[zo], e_recv.at[zo], tensor=1 - core)

    def c_copy(zo, slot):
        return remote(CSs.at[zo], CSr.at[slot], c_send.at[zo], c_recv.at[slot], expert=zo * nx + x)

    def forward_z(zo, k):
        @pl.when(jnp.logical_and(zo <= z, z + 1 < nz))
        def _():
            z_copy(zo, 0, k).start()

        @pl.when(jnp.logical_and(zo >= z, z >= 1))
        def _():
            z_copy(zo, 1, k).start()

    def take_z(zo):
        for k in range(chunks):
            z_copy(zo, 0, k).wait_recv()
            forward_z(zo, k)

    def spread(zo):
        e = zo * nx + x
        r = lax.broadcasted_iota(jnp.int32, (cap, rows), 0)
        near = jnp.where(r < ch, r + core * ch, r - ch + (1 - core) * ch).astype(f32)
        pick = jnp.concatenate([jnp.where(r.astype(f32) == POS[pl.ds(n + e, 1), :], 1.0, 0.0),
                                jnp.where(near == POS[pl.ds(e, 1), :], 1.0, 0.0)], axis=0).astype(bf)
        got = jnp.dot(pick, X[zo], preferred_element_type=f32).astype(bf)
        XC[zo] = got[:cap]
        for k in range(2):
            x_copy(zo, k, core).start()
        XIN[zo, core, :ch] = got[cap:cap + ch]
        XO[zo] = got[cap + ch:]
        d_copy(zo, core).start()

    for d in range(1, n):
        m_copy(me, d).start()
    for k in range(chunks):
        forward_z(z, k)
    spread(z)
    rem_w = [remote(a.at[0], b.at[1], w_send.at[i], w_recv.at[i], tensor=1 - core) for i, (a, b) in enumerate(
        ((wg_ref, Wg), (wu_ref, Wu), (wd_ref, Wd)))]
    for cp in rem_w:
        cp.start()

    table = [sorted(range(nz), key=lambda q: (abs(q - k), abs(2 * q + 1 - nz))) for k in range(nz)]

    def nth(i):
        r = table[0][i]
        for k in range(1, nz):
            r = jnp.where(z == k, table[k][i], r)
        return r

    for cp in loc_s:
        cp.wait()
    tok = TOK[...]
    sh = silu_mul(jnp.dot(tok, Sg[...], preferred_element_type=f32),
                  jnp.dot(tok, Su[...], preferred_element_type=f32))
    sh_all = jnp.dot(sh, Sd[...], preferred_element_type=f32)
    SHB[0] = sh_all[:, :half]
    SHB[1] = sh_all[:, half:]
    h_copy = remote(SHB.at[1 - core], SHr, h_send, h_recv, tensor=1 - core)
    h_copy.start()

    for d in range(1, n):
        m_copy((me + d) % n, d).wait_recv()
    place, weight = ranks(MT[:, :top], MT[:, top:])
    POS[...] = place
    WT[...] = weight
    PCOL[...] = place.T

    for cp in loc_w:
        cp.wait()
    for cp in rem_w:
        cp.wait_recv()

    def compute(zo):
        d_copy(zo, 1 - core).wait_recv()
        for s in range(2):
            x_copy(zo, s, s).wait_recv()
        for hh in range(2):
            parts = []
            for w in (Wg, Wu):
                parts.append(jnp.dot(XIN[zo, 0], w[hh, :half], preferred_element_type=f32)
                             + jnp.dot(XIN[zo, 1], w[hh, half:], preferred_element_type=f32))
            down = jnp.dot(silu_mul(*parts), Wd[hh], preferred_element_type=f32)
            if hh == 0:
                O[...] = down
            else:
                O[...] += down
        r = (lax.broadcasted_iota(jnp.int32, (ch, rows), 0) + core * ch).astype(f32)
        weight = jnp.concatenate(
            [jnp.sum(jnp.where(r == POS[pl.ds(e, 1), :], WT[pl.ds(e, 1), :], 0.0), axis=1, keepdims=True)
             for e in (zo * nx + x, zo * nx + ox)], axis=0)
        y = (weight * O[...].astype(bf).astype(f32)).astype(bf)
        YS[zo, 0] = y[:, :half]
        YS[zo, 1] = y[:, half:]

    def give_near(zo):
        e_copy(zo, core).start()
        YC[zo, pl.ds(pl.multiple_of(core * ch, ch), ch)] = YS[zo, core, :ch]

    def give_far(zo):
        for k in range(2):
            y_copy(zo, k, core).start()

    def column(zo):
        e_copy(zo, 1 - core).wait_recv()
        for s in range(2):
            y_copy(zo, s, s).wait_recv()
        e = zo * nx + x
        lane = lax.broadcasted_iota(jnp.int32, PCOL.shape, 1)
        mine = jnp.sum(jnp.where(lane == e, PCOL[...], 0.0), axis=1, keepdims=True)
        theirs = jnp.sum(jnp.where(lane == n + e, PCOL[...], 0.0), axis=1, keepdims=True)
        theirs = jnp.where(theirs < 0, -1.0, theirs + cap)
        slot = lax.broadcasted_iota(jnp.int32, (rows, 2 * cap), 1)
        put = jnp.where(slot.astype(f32) == jnp.where(slot < cap, mine, theirs), 1.0, 0.0).astype(bf)
        return jnp.dot(put, YC[zo], preferred_element_type=f32)

    def column_sum(zo):
        CSs[zo] = column(zo).astype(bf)
        c_copy(zo, z).start()

    edge = jnp.logical_or(z == 0, z == nz - 1)
    for i in range(nz):
        zi = nth(i)

        @pl.when(edge)
        def _():
            if i + 1 < nz:
                take_z(nth(i + 1))
                spread(nth(i + 1))

        @pl.when(jnp.logical_not(edge))
        def _():
            if i == 0:
                for j in range(1, min(3, nz)):
                    take_z(nth(j))
                    spread(nth(j))
            elif i + 2 < nz:
                take_z(nth(i + 2))
                spread(nth(i + 2))
        if i >= 3:
            column_sum(nth(i - 2))
        compute(zi)
        give_near(zi)
        if i > 0:
            give_far(zi)
    give_far(z)
    for i in range(max(1, nz - 2), nz):
        column_sum(nth(i))
    OWN[...] = column(z)
    h_copy.wait_recv()
    total = X[z].astype(f32) + OWN[...] + (SHB[core] + SHr[...])
    for i in range(1, nz):
        zi = nth(i)
        c_copy(zi, zi).wait_recv()
        total = total + CSr[zi].astype(f32)
    out_ref[...] = total.astype(bf)

    for cp in rem_w:
        cp.wait_send()
    h_copy.wait_send()
    for d in range(1, n):
        m_copy(me, d).wait_send()
    for zo in range(nz):
        for k in range(chunks):
            @pl.when(jnp.logical_and(zo <= z, z + 1 < nz))
            def _():
                z_copy(zo, 0, k).wait_send()

            @pl.when(jnp.logical_and(zo >= z, z >= 1))
            def _():
                z_copy(zo, 1, k).wait_send()
        for k in range(2):
            x_copy(zo, k, core).wait_send()
            y_copy(zo, k, core).wait_send()
        d_copy(zo, core).wait_send()
        e_copy(zo, core).wait_send()

        @pl.when(zo != z)
        def _():
            c_copy(zo, z).wait_send()


def pad(n, m):
    return -(-n // m) * m


def most_named(tok_count, top_count, experts_all):
    return max(2, (3 * tok_count * top_count + 2 * experts_all - 1) // (2 * experts_all))


def gather_plan(tok_count, width, expert_count, local_experts, hidden, top_count):
    cap = most_named(tok_count, top_count, expert_count)
    if local_experts != 1 or expert_count % 2 or tok_count % 256 or width % 32 or cap % 32 or cap > tok_count:
        return None
    nz, half = expert_count // 2, pad(width // 2, 128)
    wide, hid = pad(width, 128), pad(hidden, 128)
    weights = 3 * (2 * width * hid + pad(hidden, 16) * wide) * 2
    moved = nz * half * 2 * (3 * tok_count + 2 * cap + 2 * cap + 2 * cap + 2 * cap)
    flat = tok_count * (wide * 2 + 4 * half * 4 + 2 * half) + cap * wide * 4 + 4 * tok_count * tok_count
    return weights + moved + flat


def gather_local(tokens, routes, gates, w_gate, w_up, w_down, shared_gate, shared_up, shared_down):
    tok_count, width = tokens.shape
    hidden = w_gate.shape[2]
    n = lax.axis_size("expert")
    top = routes.shape[1]
    nx, nz = 2, n // 2
    half = width // 2
    cap = most_named(tok_count, top, n)
    ch = cap // 2
    chunks = 2
    bf, f32 = jnp.bfloat16, jnp.float32
    vm, dma = pltpu.VMEM, pltpu.SemaphoreType.DMA
    scratch = [
        vm((tok_count, width), bf), vm((nz, tok_count, half), bf), vm((nz, cap, half), bf), vm((nz, ch, half), bf),
        vm((nz, 2, cap, half), bf), vm((nz, 2, cap, half), bf), vm((nz, 2 * cap, half), bf),
        vm((nz, tok_count, half), bf), vm((nz, tok_count, half), bf), vm((tok_count, half), f32),
        vm((cap, width), f32), vm((2, tok_count, half), f32), vm((tok_count, half), f32),
        vm((n, 2 * top, tok_count), f32), vm((2 * n, tok_count), f32), vm((n, tok_count), f32),
        vm((tok_count, 2 * n), f32), vm((tok_count, tok_count), bf),
        vm((2, width, hidden), bf), vm((2, width, hidden), bf), vm((2, hidden, width), bf),
        vm((width, hidden), bf), vm((width, hidden), bf), vm((hidden, width), bf),
        dma, dma((3,)), dma((3,)), dma((3,)), dma((3,)), dma((n,)), dma((n,)),
        dma((2, nz, chunks)), dma((nz, chunks)), dma((2, nz)), dma((2, nz)), dma((nz,)), dma((nz,)),
        dma((2, nz)), dma((2, nz)), dma((nz,)), dma((nz,)), dma((nz,)), dma((nz,)), dma, dma,
    ]
    in_vmem, in_hbm = pl.BlockSpec(memory_space=pltpu.VMEM), pl.BlockSpec(memory_space=pl.ANY)
    return pl.pallas_call(
        functools.partial(moe_kernel, nz, nx, cap),
        out_shape=jax.ShapeDtypeStruct((tok_count, half), bf),
        in_specs=[in_hbm] + [in_vmem] * 2 + [in_hbm] * 6,
        out_specs=in_vmem,
        scratch_shapes=scratch,
        compiler_params=pltpu.CompilerParams(collective_id=0, has_side_effects=True, vmem_limit_bytes=60 * 1024 * 1024),
    )(tokens, routes.T, gates.T, w_gate, w_up, w_down, shared_gate, shared_up, shared_down)


def local(tokens, routes, gates, w_gate, *rest):
    need = gather_plan(*tokens.shape, lax.axis_size("expert"), w_gate.shape[0], w_gate.shape[2], routes.shape[1])
    if need is not None and lax.axis_size("tensor") == 2 and need <= VMEM_BUDGET:
        return gather_local(tokens, routes, gates, w_gate, *rest)
    return exchange_local(tokens, routes, gates, w_gate, *rest)


def solution(mesh):
    in_specs = (
        P(("groups", "expert"), None),
        P(("groups", "expert"), None),
        P(("groups", "expert"), None),
        P("expert", None, "tensor"),
        P("expert", None, "tensor"),
        P("expert", "tensor", None),
        P(None, "tensor"),
        P(None, "tensor"),
        P("tensor", None),
    )
    out_specs = P(("groups", "expert"), "tensor")
    return jax.shard_map(local, mesh=mesh, in_specs=in_specs, out_specs=out_specs, check_vma=False)
```

time: 93.7 us -> 90.4 us (0.965)
  Pallas kernels: 89.3 us -> 85.6 us
    pallas_call x1, Pallas kernels: 89.3 us -> 85.6 us  [gather_local(): pl.pallas_call(functools.partial(moe_kernel, nz, nx, cap), out_shape=jax....]
where the time goes in v1:
time: 90.4 us; the launch traced here: 89.8 us
  Pallas kernels  85.6 us (95%)
  local copies, waits for them, and re-layouts  4.17 us (5%)
    pallas_call x1, Pallas kernels, gather_local(): pl.pallas_call(functools.partial(moe_kernel, nz, nx, cap), out_shape=jax....  85.6 us
    unnamed x1, local copies, waits for them, and re-layouts  2.27 us
    pallas_call x1, local copies, waits for them, and re-layouts, gather_local(): pl.pallas_call(functools.partial(moe_kernel, nz, nx, cap), out_shape=jax....  1.91 us

profile of v1, /device:TPU:1, one launch (start us, length us, event | category | flops | bytes accessed | tf_op | source)
XLA Modules:
  0.0 89.8 jit_solution(17547787540240546909)
XLA Ops:
  0.0 2.3 %copy.10.tok_ref = bf16[256,1440]{1,0:T(8,128)(2,1)} copy(bf16[256,1440]{0,1:T(8,128)(2,1)} %param.9) | data formatting | bytes 1474560 | tf_op args[0]
  2.3 85.6 %shard_map.91 = bf16[256,720]{1,0:T(8,128)(2,1)} custom-call(bf16[256,1440]{1,0:T(8,128)(2,1)} %copy.10.tok_ref, s32[4,256]{1,0:T(4,128)} %bitcast.2, f32[4,256]{1,0:T(4,128)} %bitcast.3, bf16[1,1440,720]{2,1,0:T(8,128)(2,1)} %wg_ref.1, bf16[1,1440,720]{2,1,0:T(8,128)(2,1)} %wu_ref.1, bf16[1,720,1440]{2,1,0:T(8,128)(2,1)} %wd_ref.1, ...), custom_call_target="tpu_custom_call" | custom-call | tf_op jit(solution)/shard_map/pallas_call | solution.py:377
  87.9 1.9 %copy.11 = bf16[256,720]{0,1:T(8,128)(2,1)} copy(bf16[256,720]{1,0:T(8,128)(2,1)} %shard_map.91) | data formatting | bytes 737280 | tf_op jit(solution)/shard_map/pallas_call | solution.py:377

commit v2 on v1

--- a/solution.py
+++ b/solution.py
@@ -64,7 +64,7 @@
 
 
 def moe_kernel(nz, nx, cap, tok_ref, routes_ref, gates_ref, wg_ref, wu_ref, wd_ref, sg_ref, su_ref, sd_ref, out_ref,
-               TOK, X, XC, XO, XIN, YS, YC, CSs, CSr, OWN, O, SHB, SHr, MT, POS, WT, PCOL, U, Wg, Wu, Wd, Sg, Su, Sd,
+               TOK, X, XC, XO, XIN, YS, YC, CSs, CSr, OWN, O, SHB, SHr, MT, POS, WT, U, Wg, Wu, Wd, Sg, Su, Sd,
                t_loc, w_loc, s_loc, w_send, w_recv, m_send, m_recv, z_send, z_recv, x_send, x_recv, d_send, d_recv,
                y_send, y_recv, e_send, e_recv, c_send, c_recv, h_send, h_recv):
     bf, f32 = jnp.bfloat16, jnp.float32
@@ -75,12 +75,11 @@
     ox = nx - 1 - x
     other = z * nx + ox
     n = nz * nx
-    rows = X.shape[1]
-    half = out_ref.shape[1]
+    half, rows = out_ref.shape
     ch = cap // 2
     top = routes_ref.shape[0]
     chunks = z_recv.shape[1]
-    part = rows // chunks
+    part = half // chunks
 
     barrier = pltpu.get_barrier_semaphore()
     for d in range(1, n):
@@ -88,7 +87,9 @@
     pl.semaphore_signal(barrier, inc=1, device_id={"tensor": 1 - core}, device_id_type=MESH)
     pl.semaphore_signal(barrier, inc=1, device_id={"expert": other, "tensor": 1 - core}, device_id_type=MESH)
 
-    tok_in = pltpu.make_async_copy(tok_ref, TOK, t_loc)
+    own_in = pltpu.make_async_copy(tok_ref.at[pl.ds(pl.multiple_of(core * half, 16), half)], X.at[z], t_loc.at[0])
+    tok_in = pltpu.make_async_copy(tok_ref, TOK, t_loc.at[1])
+    own_in.start()
     tok_in.start()
     loc_s = [pltpu.make_async_copy(a, b, s_loc.at[i]) for i, (a, b) in enumerate(
         ((sg_ref, Sg), (su_ref, Su), (sd_ref, Sd)))]
@@ -116,11 +117,7 @@
     place, _ = ranks(routes_ref[...].astype(f32)[None], gates_ref[...][None])
     POS[pl.ds(me, 1), :] = place[:1]
     POS[pl.ds(n + me, 1), :] = place[1:]
-    tok_in.wait()
-    for cc in range(2):
-        @pl.when(core == cc)
-        def _():
-            X[z] = TOK[:, cc * half:(cc + 1) * half]
+    own_in.wait()
     pl.semaphore_wait(barrier, n + 1)
 
     def m_copy(e, d):
@@ -170,7 +167,7 @@
         near = jnp.where(r < ch, r + core * ch, r - ch + (1 - core) * ch).astype(f32)
         pick = jnp.concatenate([jnp.where(r.astype(f32) == POS[pl.ds(n + e, 1), :], 1.0, 0.0),
                                 jnp.where(near == POS[pl.ds(e, 1), :], 1.0, 0.0)], axis=0).astype(bf)
-        got = jnp.dot(pick, X[zo], preferred_element_type=f32).astype(bf)
+        got = lax.dot_general(pick, X[zo], (((1,), (1,)), ((), ())), preferred_element_type=f32).astype(bf)
         XC[zo] = got[:cap]
         for k in range(2):
             x_copy(zo, k, core).start()
@@ -198,12 +195,13 @@
 
     for cp in loc_s:
         cp.wait()
-    tok = TOK[...]
+    tok_in.wait()
+    tok = TOK[...].T
     sh = silu_mul(jnp.dot(tok, Sg[...], preferred_element_type=f32),
                   jnp.dot(tok, Su[...], preferred_element_type=f32))
-    sh_all = jnp.dot(sh, Sd[...], preferred_element_type=f32)
-    SHB[0] = sh_all[:, :half]
-    SHB[1] = sh_all[:, half:]
+    sh_all = jnp.dot(sh, Sd[...], preferred_element_type=f32).T
+    SHB[0] = sh_all[:half]
+    SHB[1] = sh_all[half:]
     h_copy = remote(SHB.at[1 - core], SHr, h_send, h_recv, tensor=1 - core)
     h_copy.start()
 
@@ -212,7 +210,6 @@
     place, weight = ranks(MT[:, :top], MT[:, top:])
     POS[...] = place
     WT[...] = weight
-    PCOL[...] = place.T
 
     for cp in loc_w:
         cp.wait()
@@ -254,13 +251,9 @@
         for s in range(2):
             y_copy(zo, s, s).wait_recv()
         e = zo * nx + x
-        lane = lax.broadcasted_iota(jnp.int32, PCOL.shape, 1)
-        mine = jnp.sum(jnp.where(lane == e, PCOL[...], 0.0), axis=1, keepdims=True)
-        theirs = jnp.sum(jnp.where(lane == n + e, PCOL[...], 0.0), axis=1, keepdims=True)
-        theirs = jnp.where(theirs < 0, -1.0, theirs + cap)
-        slot = lax.broadcasted_iota(jnp.int32, (rows, 2 * cap), 1)
-        put = jnp.where(slot.astype(f32) == jnp.where(slot < cap, mine, theirs), 1.0, 0.0).astype(bf)
-        return jnp.dot(put, YC[zo], preferred_element_type=f32)
+        slot = lax.broadcasted_iota(jnp.int32, (cap, rows), 0).astype(f32)
+        put = jnp.concatenate([jnp.where(slot == POS[pl.ds(q, 1), :], 1.0, 0.0) for q in (e, n + e)], axis=0).astype(bf)
+        return lax.dot_general(YC[zo], put, (((0,), (0,)), ((), ())), preferred_element_type=f32)
 
     def column_sum(zo):
         CSs[zo] = column(zo).astype(bf)
@@ -357,31 +350,31 @@
     half = width // 2
     cap = most_named(tok_count, top, n)
     ch = cap // 2
-    chunks = 2
+    chunks = next(c for c in (3, 2, 1) if half % (16 * c) == 0)
     bf, f32 = jnp.bfloat16, jnp.float32
     vm, dma = pltpu.VMEM, pltpu.SemaphoreType.DMA
     scratch = [
-        vm((tok_count, width), bf), vm((nz, tok_count, half), bf), vm((nz, cap, half), bf), vm((nz, ch, half), bf),
+        vm((width, tok_count), bf), vm((nz, half, tok_count), bf), vm((nz, cap, half), bf), vm((nz, ch, half), bf),
         vm((nz, 2, cap, half), bf), vm((nz, 2, cap, half), bf), vm((nz, 2 * cap, half), bf),
-        vm((nz, tok_count, half), bf), vm((nz, tok_count, half), bf), vm((tok_count, half), f32),
-        vm((cap, width), f32), vm((2, tok_count, half), f32), vm((tok_count, half), f32),
+        vm((nz, half, tok_count), bf), vm((nz, half, tok_count), bf), vm((half, tok_count), f32),
+        vm((cap, width), f32), vm((2, half, tok_count), f32), vm((half, tok_count), f32),
         vm((n, 2 * top, tok_count), f32), vm((2 * n, tok_count), f32), vm((n, tok_count), f32),
-        vm((tok_count, 2 * n), f32), vm((tok_count, tok_count), bf),
+        vm((tok_count, tok_count), bf),
         vm((2, width, hidden), bf), vm((2, width, hidden), bf), vm((2, hidden, width), bf),
         vm((width, hidden), bf), vm((width, hidden), bf), vm((hidden, width), bf),
-        dma, dma((3,)), dma((3,)), dma((3,)), dma((3,)), dma((n,)), dma((n,)),
+        dma((2,)), dma((3,)), dma((3,)), dma((3,)), dma((3,)), dma((n,)), dma((n,)),
         dma((2, nz, chunks)), dma((nz, chunks)), dma((2, nz)), dma((2, nz)), dma((nz,)), dma((nz,)),
         dma((2, nz)), dma((2, nz)), dma((nz,)), dma((nz,)), dma((nz,)), dma((nz,)), dma, dma,
     ]
     in_vmem, in_hbm = pl.BlockSpec(memory_space=pltpu.VMEM), pl.BlockSpec(memory_space=pl.ANY)
     return pl.pallas_call(
         functools.partial(moe_kernel, nz, nx, cap),
-        out_shape=jax.ShapeDtypeStruct((tok_count, half), bf),
+        out_shape=jax.ShapeDtypeStruct((half, tok_count), bf),
         in_specs=[in_hbm] + [in_vmem] * 2 + [in_hbm] * 6,
         out_specs=in_vmem,
         scratch_shapes=scratch,
         compiler_params=pltpu.CompilerParams(collective_id=0, has_side_effects=True, vmem_limit_bytes=60 * 1024 * 1024),
-    )(tokens, routes.T, gates.T, w_gate, w_up, w_down, shared_gate, shared_up, shared_down)
+    )(tokens.T, routes.T, gates.T, w_gate, w_up, w_down, shared_gate, shared_up, shared_down).T
 
 
 def local(tokens, routes, gates, w_gate, *rest):

time: 90.4 us -> 85.5 us (0.946)
  local copies, waits for them, and re-layouts: 4.17 us -> 1.75 us
  Pallas kernels: 85.6 us -> 83.2 us
    pallas_call x1, Pallas kernels: 85.6 us -> 83.2 us  [gather_local(): pl.pallas_call(functools.partial(moe_kernel, nz, nx, cap), out_shape=jax....]
    pallas_call x1 -> x0, local copies, waits for them, and re-layouts: 1.91 us -> none  [gather_local(): pl.pallas_call(functools.partial(moe_kernel, nz, nx, cap), out_shape=jax....]
where the time goes in v2:
time: 85.5 us; the launch traced here: 85 us
  Pallas kernels  83.2 us (97%)
  local copies, waits for them, and re-layouts  1.75 us (2%)
    pallas_call x1, Pallas kernels, gather_local(): pl.pallas_call(functools.partial(moe_kernel, nz, nx, cap), out_shape=jax....  83.2 us
    unnamed x1, local copies, waits for them, and re-layouts  1.75 us

profile of v2, /device:TPU:1, one launch (start us, length us, event | category | flops | bytes accessed | tf_op | source)
XLA Modules:
  0.0 85.0 jit_solution(10864459779749473496)
XLA Ops:
  0.0 83.2 %shard_map.91 = bf16[720,256]{1,0:T(8,128)(2,1)} custom-call(bf16[1440,256]{1,0:T(8,128)(2,1)} %bitcast.5, s32[4,256]{1,0:T(4,128)} %bitcast.6, f32[4,256]{1,0:T(4,128)} %bitcast.7, bf16[1,1440,720]{2,1,0:T(8,128)(2,1)} %wg_ref.1, bf16[1,1440,720]{2,1,0:T(8,128)(2,1)} %wu_ref.1, bf16[1,720,1440]{2,1,0:T(8,128)(2,1)} %wd_ref.1, bf16[1440,720]{1,0:T(8,128)(2,1)} %sg_ref.1, ...), custom_call_target="tpu_custom_call" | custom-call | tf_op jit(solution)/shard_map/pallas_call | solution.py:370
  83.2 1.7 %copy.11 = bf16[256,720]{0,1:T(8,128)(2,1)} copy(bf16[256,720]{0,1:T(8,128)(2,1)} %bitcast.4) | data formatting | bytes 737280

commit v3 on v2

--- a/solution.py
+++ b/solution.py
@@ -9,6 +9,18 @@
 
 MESH = pl.DeviceIdType.MESH
 VMEM_BUDGET = 52 * 1024 * 1024
+LINE = 4
+EDGE_ORDER = (
+    ("take", 1), ("spread", 1), ("take", 2), ("spread", 2), ("compute", 0), ("take", 3), ("spread", 3),
+    ("compute", 2), ("give", 2), ("compute", 3), ("compute", 1), ("give", 3), ("give", 1), ("sum", 2), ("sum",
+    3), ("sum", 1), ("give", 0), ("sum", 0),
+)
+INNER_ORDER = (
+    ("take", 1), ("spread", 1), ("take", 2), ("spread", 2), ("take", 3), ("spread", 3), ("compute", 0),
+    ("compute", 1), ("compute", 2), ("give", 2), ("give", 1), ("sum", 2), ("compute", 3), ("give", 3),
+    ("give", 0), ("sum", 1), ("sum", 3), ("sum", 0),
+)
+RELAYED, MERGED, SOURCES = (2, 3), (1, 3), (1, 2)
 
 
 def exchange_local(tokens, routes, gates, w_gate, w_up, w_down, shared_gate, shared_up, shared_down):
@@ -64,9 +76,9 @@
 
 
 def moe_kernel(nz, nx, cap, tok_ref, routes_ref, gates_ref, wg_ref, wu_ref, wd_ref, sg_ref, su_ref, sd_ref, out_ref,
-               TOK, X, XC, XO, XIN, YS, YC, CSs, CSr, OWN, O, SHB, SHr, MT, POS, WT, U, Wg, Wu, Wd, Sg, Su, Sd,
+               TOK, X, XC, XO, XIN, YS, YC, CSs, CSr, MRG, OWN, O, SHB, SHr, MT, POS, WT, U, Wg, Wu, Wd, Sg, Su, Sd,
                t_loc, w_loc, s_loc, w_send, w_recv, m_send, m_recv, z_send, z_recv, x_send, x_recv, d_send, d_recv,
-               y_send, y_recv, e_send, e_recv, c_send, c_recv, h_send, h_recv):
+               y_send, y_recv, e_send, e_recv, c_send, c_recv, g_recv, h_send, h_recv):
     bf, f32 = jnp.bfloat16, jnp.float32
     me = lax.axis_index("expert")
     core = lax.axis_index("tensor")
@@ -80,6 +92,8 @@
     top = routes_ref.shape[0]
     chunks = z_recv.shape[1]
     part = half // chunks
+    sum_chunks = c_send.shape[1]
+    sum_part = half // sum_chunks
 
     barrier = pltpu.get_barrier_semaphore()
     for d in range(1, n):
@@ -144,8 +158,14 @@
         r = pl.ds(pl.multiple_of(source * ch, ch), ch)
         return remote(YS.at[zo, 1 - core, pl.ds(0, ch)], YC.at[zo, r], e_send.at[zo], e_recv.at[zo], tensor=1 - core)
 
-    def c_copy(zo, slot):
-        return remote(CSs.at[zo], CSr.at[slot], c_send.at[zo], c_recv.at[slot], expert=zo * nx + x)
+    def c_copy(zo, slot, k):
+        r = pl.ds(k * sum_part, sum_part)
+        return remote(CSs.at[zo, r], CSr.at[slot, r], c_send.at[zo, k], c_recv.at[slot, k], expert=zo * nx + x)
+
+    def g_copy(zo, k):
+        r = pl.ds(k * sum_part, sum_part)
+        return remote(CSs.at[zo, r], MRG.at[zo, r], c_send.at[zo, k], g_recv.at[zo, k],
+                      expert=jnp.where(z == 0, me + nx, me - nx))
 
     def forward_z(zo, k):
         @pl.when(jnp.logical_and(zo <= z, z + 1 < nz))
@@ -255,46 +275,71 @@
         put = jnp.concatenate([jnp.where(slot == POS[pl.ds(q, 1), :], 1.0, 0.0) for q in (e, n + e)], axis=0).astype(bf)
         return lax.dot_general(YC[zo], put, (((0,), (0,)), ((), ())), preferred_element_type=f32)
 
-    def column_sum(zo):
-        CSs[zo] = column(zo).astype(bf)
-        c_copy(zo, z).start()
+    def column_sum(i, on_edge):
+        zo = nth(i)
+        if i == 0:
+            OWN[...] = X[z].astype(f32) + column(z)
+            return
+        summed = column(zo)
+        for k in range(sum_chunks):
+            r = slice(k * sum_part, (k + 1) * sum_part)
+            piece = summed[r]
+            if not on_edge and i in MERGED:
+                g_copy(zo, k).wait_recv()
+                piece = piece + MRG[zo, r].astype(f32)
+            CSs[zo, r] = piece.astype(bf)
+            if on_edge and i in RELAYED:
+                g_copy(zo, k).start()
+            else:
+                c_copy(zo, z, k).start()
 
     edge = jnp.logical_or(z == 0, z == nz - 1)
-    for i in range(nz):
-        zi = nth(i)
-
+
+    def run(steps, on_edge):
+        for op, i in steps:
+            if op == "take":
+                take_z(nth(i))
+            elif op == "spread":
+                spread(nth(i))
+            elif op == "give":
+                give_far(nth(i))
+            else:
+                column_sum(i, on_edge)
+
+    def cut(order):
+        gaps, firsts = [[]], []
+        for op, i in order:
+            if op == "compute":
+                firsts.append(i)
+                gaps.append([])
+            else:
+                gaps[-1].append((op, i))
+        return gaps, firsts
+
+    edge_gaps, edge_first = cut(EDGE_ORDER)
+    inner_gaps, inner_first = cut(INNER_ORDER)
+    for j in range(nz + 1):
         @pl.when(edge)
         def _():
-            if i + 1 < nz:
-                take_z(nth(i + 1))
-                spread(nth(i + 1))
+            run(edge_gaps[j], True)
 
         @pl.when(jnp.logical_not(edge))
         def _():
-            if i == 0:
-                for j in range(1, min(3, nz)):
-                    take_z(nth(j))
-                    spread(nth(j))
-            elif i + 2 < nz:
-                take_z(nth(i + 2))
-                spread(nth(i + 2))
-        if i >= 3:
-            column_sum(nth(i - 2))
-        compute(zi)
-        give_near(zi)
-        if i > 0:
-            give_far(zi)
-    give_far(z)
-    for i in range(max(1, nz - 2), nz):
-        column_sum(nth(i))
-    OWN[...] = column(z)
+            run(inner_gaps[j], False)
+        if j < nz:
+            zi = jnp.where(edge, nth(edge_first[j]), nth(inner_first[j]))
+            compute(zi)
+            give_near(zi)
     h_copy.wait_recv()
-    total = X[z].astype(f32) + OWN[...] + (SHB[core] + SHr[...])
-    for i in range(1, nz):
-        zi = nth(i)
-        c_copy(zi, zi).wait_recv()
-        total = total + CSr[zi].astype(f32)
-    out_ref[...] = total.astype(bf)
+    OWN[...] += SHB[core] + SHr[...]
+    for k in range(sum_chunks):
+        r = slice(k * sum_part, (k + 1) * sum_part)
+        total = OWN[r]
+        for i in SOURCES:
+            zi = nth(i)
+            c_copy(zi, zi, k).wait_recv()
+            total = total + CSr[zi, r].astype(f32)
+        out_ref[r] = total.astype(bf)
 
     for cp in rem_w:
         cp.wait_send()
@@ -318,7 +363,8 @@
 
         @pl.when(zo != z)
         def _():
-            c_copy(zo, z).wait_send()
+            for k in range(sum_chunks):
+                c_copy(zo, z, k).wait_send()
 
 
 def pad(n, m):
@@ -331,12 +377,12 @@
 
 def gather_plan(tok_count, width, expert_count, local_experts, hidden, top_count):
     cap = most_named(tok_count, top_count, expert_count)
-    if local_experts != 1 or expert_count % 2 or tok_count % 256 or width % 32 or cap % 32 or cap > tok_count:
+    if local_experts != 1 or expert_count != 2 * LINE or tok_count % 256 or width % 32 or cap % 32 or cap > tok_count:
         return None
     nz, half = expert_count // 2, pad(width // 2, 128)
     wide, hid = pad(width, 128), pad(hidden, 128)
     weights = 3 * (2 * width * hid + pad(hidden, 16) * wide) * 2
-    moved = nz * half * 2 * (3 * tok_count + 2 * cap + 2 * cap + 2 * cap + 2 * cap)
+    moved = nz * half * 2 * (4 * tok_count + 2 * cap + 2 * cap + 2 * cap + 2 * cap)
     flat = tok_count * (wide * 2 + 4 * half * 4 + 2 * half) + cap * wide * 4 + 4 * tok_count * tok_count
     return weights + moved + flat
 
@@ -351,12 +397,13 @@
     cap = most_named(tok_count, top, n)
     ch = cap // 2
     chunks = next(c for c in (3, 2, 1) if half % (16 * c) == 0)
+    sums = chunks
     bf, f32 = jnp.bfloat16, jnp.float32
     vm, dma = pltpu.VMEM, pltpu.SemaphoreType.DMA
     scratch = [
         vm((width, tok_count), bf), vm((nz, half, tok_count), bf), vm((nz, cap, half), bf), vm((nz, ch, half), bf),
         vm((nz, 2, cap, half), bf), vm((nz, 2, cap, half), bf), vm((nz, 2 * cap, half), bf),
-        vm((nz, half, tok_count), bf), vm((nz, half, tok_count), bf), vm((half, tok_count), f32),
+        vm((nz, half, tok_count), bf), vm((nz, half, tok_count), bf), vm((nz, half, tok_count), bf), vm((half, tok_count), f32),
         vm((cap, width), f32), vm((2, half, tok_count), f32), vm((half, tok_count), f32),
         vm((n, 2 * top, tok_count), f32), vm((2 * n, tok_count), f32), vm((n, tok_count), f32),
         vm((tok_count, tok_count), bf),
@@ -364,7 +411,7 @@
         vm((width, hidden), bf), vm((width, hidden), bf), vm((hidden, width), bf),
         dma((2,)), dma((3,)), dma((3,)), dma((3,)), dma((3,)), dma((n,)), dma((n,)),
         dma((2, nz, chunks)), dma((nz, chunks)), dma((2, nz)), dma((2, nz)), dma((nz,)), dma((nz,)),
-        dma((2, nz)), dma((2, nz)), dma((nz,)), dma((nz,)), dma((nz,)), dma((nz,)), dma, dma,
+        dma((2, nz)), dma((2, nz)), dma((nz,)), dma((nz,)), dma((nz, sums)), dma((nz, sums)), dma((nz, sums)), dma, dma,
     ]
     in_vmem, in_hbm = pl.BlockSpec(memory_space=pltpu.VMEM), pl.BlockSpec(memory_space=pl.ANY)
     return pl.pallas_call(

time: 85.5 us -> 77.1 us (0.902)
  Pallas kernels: 83.2 us -> 75.2 us
    pallas_call x1, Pallas kernels: 83.2 us -> 75.2 us  [gather_local(): pl.pallas_call(functools.partial(moe_kernel, nz, nx, cap), out_shape=jax....]
where the time goes in v3:
time: 77.1 us; the launch traced here: 76.9 us
  Pallas kernels  75.2 us (98%)
  local copies, waits for them, and re-layouts  1.75 us (2%)
    pallas_call x1, Pallas kernels, gather_local(): pl.pallas_call(functools.partial(moe_kernel, nz, nx, cap), out_shape=jax....  75.2 us
    unnamed x1, local copies, waits for them, and re-layouts  1.75 us

profile of v3, /device:TPU:1, one launch (start us, length us, event | category | flops | bytes accessed | tf_op | source)
XLA Modules:
  0.0 76.9 jit_solution(16744980220559802735)
XLA Ops:
  0.0 75.2 %shard_map.91 = bf16[720,256]{1,0:T(8,128)(2,1)} custom-call(bf16[1440,256]{1,0:T(8,128)(2,1)} %bitcast.5, s32[4,256]{1,0:T(4,128)} %bitcast.6, f32[4,256]{1,0:T(4,128)} %bitcast.7, bf16[1,1440,720]{2,1,0:T(8,128)(2,1)} %wg_ref.1, bf16[1,1440,720]{2,1,0:T(8,128)(2,1)} %wu_ref.1, bf16[1,720,1440]{2,1,0:T(8,128)(2,1)} %wd_ref.1, bf16[1440,720]{1,0:T(8,128)(2,1)} %sg_ref.1, ...), custom_call_target="tpu_custom_call" | custom-call | tf_op jit(solution)/shard_map/pallas_call | solution.py:417
  75.2 1.7 %copy.11 = bf16[256,720]{0,1:T(8,128)(2,1)} copy(bf16[256,720]{0,1:T(8,128)(2,1)} %bitcast.4) | data formatting | bytes 737280

commit v4 on v3

--- a/solution.py
+++ b/solution.py
@@ -11,13 +11,13 @@
 VMEM_BUDGET = 52 * 1024 * 1024
 LINE = 4
 EDGE_ORDER = (
-    ("take", 1), ("spread", 1), ("take", 2), ("spread", 2), ("compute", 0), ("take", 3), ("spread", 3),
-    ("compute", 2), ("give", 2), ("compute", 3), ("compute", 1), ("give", 3), ("give", 1), ("sum", 2), ("sum",
-    3), ("sum", 1), ("give", 0), ("sum", 0),
+    ("take", 1), ("spread", 1), ("compute", 0), ("take", 2), ("spread", 2), ("compute", 1), ("sum", 1),
+    ("take", 3), ("spread", 3), ("compute", 2), ("give", 2), ("compute", 3), ("give", 3), ("sum", 2), ("give",
+    0), ("sum", 3), ("sum", 0),
 )
 INNER_ORDER = (
-    ("take", 1), ("spread", 1), ("take", 2), ("spread", 2), ("take", 3), ("spread", 3), ("compute", 0),
-    ("compute", 1), ("compute", 2), ("give", 2), ("give", 1), ("sum", 2), ("compute", 3), ("give", 3),
+    ("take", 1), ("spread", 1), ("take", 2), ("spread", 2), ("take", 3), ("spread", 3), ("compute", 1),
+    ("compute", 2), ("give", 2), ("compute", 0), ("give", 1), ("compute", 3), ("give", 3), ("sum", 2),
     ("give", 0), ("sum", 1), ("sum", 3), ("sum", 0),
 )
 RELAYED, MERGED, SOURCES = (2, 3), (1, 3), (1, 2)
@@ -76,9 +76,10 @@
 
 
 def moe_kernel(nz, nx, cap, tok_ref, routes_ref, gates_ref, wg_ref, wu_ref, wd_ref, sg_ref, su_ref, sd_ref, out_ref,
-               TOK, X, XC, XO, XIN, YS, YC, CSs, CSr, MRG, OWN, O, SHB, SHr, MT, POS, WT, U, Wg, Wu, Wd, Sg, Su, Sd,
-               t_loc, w_loc, s_loc, w_send, w_recv, m_send, m_recv, z_send, z_recv, x_send, x_recv, d_send, d_recv,
-               y_send, y_recv, e_send, e_recv, c_send, c_recv, g_recv, h_send, h_recv):
+               TOK, X, XC, XO, XIN, YS, YC, CSs, CSr, MRG, BS, BR, AR, OWN, O, SHB, SHr, MT, POS, WT, U, Wg, Wu, Wd, Sg, Su, Sd,
+               t_loc, w_loc, s_loc, w_send, w_recv, m_send, m_recv, q_send, q_recv, z_send, z_recv, x_send, x_recv, d_send, d_recv,
+               y_send, y_recv, e_send, e_recv, f_send, f_recv,
+               a_send, a_recv, b_send, b_recv, c_send, c_recv, g_recv, h_send, h_recv):
     bf, f32 = jnp.bfloat16, jnp.float32
     me = lax.axis_index("expert")
     core = lax.axis_index("tensor")
@@ -96,8 +97,10 @@
     sum_part = half // sum_chunks
 
     barrier = pltpu.get_barrier_semaphore()
-    for d in range(1, n):
-        pl.semaphore_signal(barrier, inc=1, device_id={"expert": (me + d) % n}, device_id_type=MESH)
+    for d in range(1, nz):
+        peer = ((z + d) % nz) * nx + x
+        pl.semaphore_signal(barrier, inc=1, device_id={"expert": peer}, device_id_type=MESH)
+    pl.semaphore_signal(barrier, inc=1, device_id={"expert": other}, device_id_type=MESH)
     pl.semaphore_signal(barrier, inc=1, device_id={"tensor": 1 - core}, device_id_type=MESH)
     pl.semaphore_signal(barrier, inc=1, device_id={"expert": other, "tensor": 1 - core}, device_id_type=MESH)
 
@@ -121,21 +124,42 @@
     U[...] = jnp.where(lax.broadcasted_iota(jnp.int32, U.shape, 0) < lax.broadcasted_iota(jnp.int32, U.shape, 1),
                        1.0, 0.0).astype(bf)
 
-    def ranks(named, gate):
+    def ranks(e):
+        named, gate = MT[e, :top], MT[e, top:]
         mine, theirs = named == me.astype(f32), named == other.astype(f32)
-        on = jnp.concatenate([jnp.sum(jnp.where(mine, 1.0, 0.0), axis=1),
-                              jnp.sum(jnp.where(theirs, 1.0, 0.0), axis=1)], axis=0)
+
+        def over(value):
+            return jnp.concatenate([jnp.sum(jnp.where(hit, value, 0.0), axis=0, keepdims=True)
+                                    for hit in (mine, theirs)], axis=0)
+        on, weight = over(1.0), over(gate)
         place = jnp.dot(on.astype(bf), U[...], preferred_element_type=f32)
-        return jnp.where(on > 0, place, -1.0), jnp.sum(jnp.where(mine, gate, 0.0), axis=1)
-
-    place, _ = ranks(routes_ref[...].astype(f32)[None], gates_ref[...][None])
-    POS[pl.ds(me, 1), :] = place[:1]
-    POS[pl.ds(n + me, 1), :] = place[1:]
+        place = jnp.where(on > 0, place, -1.0)
+        for k in range(2):
+            POS[pl.ds(k * n + e, 1), :] = place[k:k + 1]
+            WT[pl.ds(k * n + e, 1), :] = weight[k:k + 1]
+
+    ranks(me)
     own_in.wait()
-    pl.semaphore_wait(barrier, n + 1)
-
-    def m_copy(e, d):
-        return remote(MT.at[e], MT.at[e], m_send.at[d], m_recv.at[e], expert=(me + d) % n)
+    pl.semaphore_wait(barrier, nz + 2)
+
+    def m_copy(zo, side):
+        e = zo * nx + x
+        return remote(MT.at[e], MT.at[e], m_send.at[side, zo], m_recv.at[zo], expert=me + nx if side == 0 else me - nx)
+
+    def q_copy(e):
+        return remote(MT.at[e], MT.at[e], q_send, q_recv, expert=other)
+
+    def f_copy(zo, source):
+        r = pl.ds(pl.multiple_of(cap + source * ch, ch), ch)
+        return remote(YS.at[zo, 1 - core, pl.ds(ch, ch)], YC.at[zo, r], f_send, f_recv, tensor=1 - core)
+
+    def b_copy(k):
+        r = pl.ds(k * sum_part, sum_part)
+        return remote(BS.at[r], BR.at[r], b_send.at[k], b_recv.at[k], expert=jnp.where(z == 0, me + nx, me - nx))
+
+    def a_copy(k):
+        r = pl.ds(k * sum_part, sum_part)
+        return remote(BS.at[r], AR.at[r], a_send.at[k], a_recv.at[k], expert=other)
 
     def z_copy(zo, side, k):
         r = pl.ds(k * part, part)
@@ -167,16 +191,25 @@
         return remote(CSs.at[zo, r], MRG.at[zo, r], c_send.at[zo, k], g_recv.at[zo, k],
                       expert=jnp.where(z == 0, me + nx, me - nx))
 
-    def forward_z(zo, k):
+    def forward(zo, start):
         @pl.when(jnp.logical_and(zo <= z, z + 1 < nz))
         def _():
-            z_copy(zo, 0, k).start()
+            start(0)
 
         @pl.when(jnp.logical_and(zo >= z, z >= 1))
         def _():
-            z_copy(zo, 1, k).start()
+            start(1)
+
+    def forward_m(zo):
+        forward(zo, lambda side: m_copy(zo, side).start())
+
+    def forward_z(zo, k):
+        forward(zo, lambda side: z_copy(zo, side, k).start())
 
     def take_z(zo):
+        m_copy(zo, 0).wait_recv()
+        forward_m(zo)
+        ranks(zo * nx + x)
         for k in range(chunks):
             z_copy(zo, 0, k).wait_recv()
             forward_z(zo, k)
@@ -195,11 +228,15 @@
         XO[zo] = got[cap + ch:]
         d_copy(zo, core).start()
 
-    for d in range(1, n):
-        m_copy(me, d).start()
+    forward_m(z)
     for k in range(chunks):
         forward_z(z, k)
     spread(z)
+    edge = jnp.logical_or(z == 0, z == nz - 1)
+
+    @pl.when(jnp.logical_not(edge))
+    def _():
+        q_copy(me).start()
     rem_w = [remote(a.at[0], b.at[1], w_send.at[i], w_recv.at[i], tensor=1 - core) for i, (a, b) in enumerate(
         ((wg_ref, Wg), (wu_ref, Wu), (wd_ref, Wd)))]
     for cp in rem_w:
@@ -224,12 +261,6 @@
     SHB[1] = sh_all[half:]
     h_copy = remote(SHB.at[1 - core], SHr, h_send, h_recv, tensor=1 - core)
     h_copy.start()
-
-    for d in range(1, n):
-        m_copy((me + d) % n, d).wait_recv()
-    place, weight = ranks(MT[:, :top], MT[:, top:])
-    POS[...] = place
-    WT[...] = weight
 
     for cp in loc_w:
         cp.wait()
@@ -250,11 +281,7 @@
                 O[...] = down
             else:
                 O[...] += down
-        r = (lax.broadcasted_iota(jnp.int32, (ch, rows), 0) + core * ch).astype(f32)
-        weight = jnp.concatenate(
-            [jnp.sum(jnp.where(r == POS[pl.ds(e, 1), :], WT[pl.ds(e, 1), :], 0.0), axis=1, keepdims=True)
-             for e in (zo * nx + x, zo * nx + ox)], axis=0)
-        y = (weight * O[...].astype(bf).astype(f32)).astype(bf)
+        y = O[...].astype(bf)
         YS[zo, 0] = y[:, :half]
         YS[zo, 1] = y[:, half:]
 
@@ -266,21 +293,59 @@
         for k in range(2):
             y_copy(zo, k, core).start()
 
-    def column(zo):
+    def keep_far(zo):
+        f_copy(zo, core).start()
+        YC[zo, pl.ds(pl.multiple_of(cap + core * ch, ch), ch)] = YS[zo, core, ch:]
+
+    def put(rows_of):
+        slot = lax.broadcasted_iota(jnp.int32, (cap, rows), 0).astype(f32)
+        return jnp.concatenate([jnp.where(slot == POS[pl.ds(q, 1), :], WT[pl.ds(q, 1), :], 0.0)
+                                for q in rows_of], axis=0).astype(bf)
+
+    def back(values, rows_of):
+        return lax.dot_general(values, put(rows_of), (((0,), (0,)), ((), ())), preferred_element_type=f32)
+
+    def column(zo, whole):
+        e = zo * nx + x
         e_copy(zo, 1 - core).wait_recv()
+        if not whole:
+            return back(YC[zo, :cap], (e,))
         for s in range(2):
             y_copy(zo, s, s).wait_recv()
-        e = zo * nx + x
-        slot = lax.broadcasted_iota(jnp.int32, (cap, rows), 0).astype(f32)
-        put = jnp.concatenate([jnp.where(slot == POS[pl.ds(q, 1), :], 1.0, 0.0) for q in (e, n + e)], axis=0).astype(bf)
-        return lax.dot_general(YC[zo], put, (((0,), (0,)), ((), ())), preferred_element_type=f32)
+        return back(YC[zo], (e, n + e))
+
+    def others(zo):
+        f_copy(zo, 1 - core).wait_recv()
+        e = zo * nx + ox
+        q_copy(e).wait_recv()
+        ranks(e)
+        return back(YC[zo, cap:], (e,))
+
+    def give(i, on_edge):
+        if i == 0 and not on_edge:
+            dense = others(z)
+            for k in range(sum_chunks):
+                r = slice(k * sum_part, (k + 1) * sum_part)
+                b_copy(k).wait_recv()
+                BS[r] = (dense[r] + BR[r].astype(f32)).astype(bf)
+                a_copy(k).start()
+        else:
+            give_far(nth(i))
 
     def column_sum(i, on_edge):
         zo = nth(i)
+        if on_edge and i == 1:
+            BS[...] = others(zo).astype(bf)
+            for k in range(sum_chunks):
+                b_copy(k).start()
+        summed = column(zo, i != (1 if on_edge else 0))
         if i == 0:
-            OWN[...] = X[z].astype(f32) + column(z)
+            OWN[...] = X[z].astype(f32) + summed
+            if not on_edge:
+                for k in range(sum_chunks):
+                    a_copy(k).wait_recv()
+                OWN[...] += AR[...].astype(f32)
             return
-        summed = column(zo)
         for k in range(sum_chunks):
             r = slice(k * sum_part, (k + 1) * sum_part)
             piece = summed[r]
@@ -293,16 +358,16 @@
             else:
                 c_copy(zo, z, k).start()
 
-    edge = jnp.logical_or(z == 0, z == nz - 1)
-
     def run(steps, on_edge):
         for op, i in steps:
             if op == "take":
                 take_z(nth(i))
             elif op == "spread":
                 spread(nth(i))
+                if on_edge and i == 1:
+                    q_copy(nth(i) * nx + x).start()
             elif op == "give":
-                give_far(nth(i))
+                give(i, on_edge)
             else:
                 column_sum(i, on_edge)
 
@@ -330,6 +395,12 @@
             zi = jnp.where(edge, nth(edge_first[j]), nth(inner_first[j]))
             compute(zi)
             give_near(zi)
+            if edge_first[j] == 1 and inner_first[j] == 0:
+                keep_far(zi)
+            elif edge_first[j] == 1:
+                pl.when(edge)(lambda: keep_far(zi))
+            elif inner_first[j] == 0:
+                pl.when(jnp.logical_not(edge))(lambda: keep_far(zi))
     h_copy.wait_recv()
     OWN[...] += SHB[core] + SHr[...]
     for k in range(sum_chunks):
@@ -344,25 +415,38 @@
     for cp in rem_w:
         cp.wait_send()
     h_copy.wait_send()
-    for d in range(1, n):
-        m_copy(me, d).wait_send()
-    for zo in range(nz):
+    q_copy(me).wait_send()
+    f_copy(z, core).wait_send()
+
+    @pl.when(edge)
+    def _():
+        for k in range(sum_chunks):
+            b_copy(k).wait_send()
+
+    @pl.when(jnp.logical_not(edge))
+    def _():
+        for k in range(sum_chunks):
+            a_copy(k).wait_send()
+    for i in range(nz):
+        zo = nth(i)
+        forward(zo, lambda side: m_copy(zo, side).wait_send())
         for k in range(chunks):
-            @pl.when(jnp.logical_and(zo <= z, z + 1 < nz))
-            def _():
-                z_copy(zo, 0, k).wait_send()
-
-            @pl.when(jnp.logical_and(zo >= z, z >= 1))
-            def _():
-                z_copy(zo, 1, k).wait_send()
+            forward(zo, lambda side: z_copy(zo, side, k).wait_send())
         for k in range(2):
             x_copy(zo, k, core).wait_send()
-            y_copy(zo, k, core).wait_send()
         d_copy(zo, core).wait_send()
         e_copy(zo, core).wait_send()
 
-        @pl.when(zo != z)
-        def _():
+        def sent():
+            for k in range(2):
+                y_copy(zo, k, core).wait_send()
+        if i == 0:
+            pl.when(edge)(sent)
+        elif i == 1:
+            pl.when(jnp.logical_not(edge))(sent)
+        else:
+            sent()
+        if i > 0:
             for k in range(sum_chunks):
                 c_copy(zo, z, k).wait_send()
 
@@ -383,7 +467,7 @@
     wide, hid = pad(width, 128), pad(hidden, 128)
     weights = 3 * (2 * width * hid + pad(hidden, 16) * wide) * 2
     moved = nz * half * 2 * (4 * tok_count + 2 * cap + 2 * cap + 2 * cap + 2 * cap)
-    flat = tok_count * (wide * 2 + 4 * half * 4 + 2 * half) + cap * wide * 4 + 4 * tok_count * tok_count
+    flat = tok_count * (wide * 2 + 4 * half * 4 + 8 * half) + cap * wide * 4 + 4 * tok_count * tok_count
     return weights + moved + flat
 
 
@@ -403,15 +487,17 @@
     scratch = [
         vm((width, tok_count), bf), vm((nz, half, tok_count), bf), vm((nz, cap, half), bf), vm((nz, ch, half), bf),
         vm((nz, 2, cap, half), bf), vm((nz, 2, cap, half), bf), vm((nz, 2 * cap, half), bf),
-        vm((nz, half, tok_count), bf), vm((nz, half, tok_count), bf), vm((nz, half, tok_count), bf), vm((half, tok_count), f32),
+        vm((nz, half, tok_count), bf), vm((nz, half, tok_count), bf), vm((nz, half, tok_count), bf),
+        vm((half, tok_count), bf), vm((half, tok_count), bf), vm((half, tok_count), bf), vm((half, tok_count), f32),
         vm((cap, width), f32), vm((2, half, tok_count), f32), vm((half, tok_count), f32),
-        vm((n, 2 * top, tok_count), f32), vm((2 * n, tok_count), f32), vm((n, tok_count), f32),
+        vm((n, 2 * top, tok_count), f32), vm((2 * n, tok_count), f32), vm((2 * n, tok_count), f32),
         vm((tok_count, tok_count), bf),
         vm((2, width, hidden), bf), vm((2, width, hidden), bf), vm((2, hidden, width), bf),
         vm((width, hidden), bf), vm((width, hidden), bf), vm((hidden, width), bf),
-        dma((2,)), dma((3,)), dma((3,)), dma((3,)), dma((3,)), dma((n,)), dma((n,)),
+        dma((2,)), dma((3,)), dma((3,)), dma((3,)), dma((3,)), dma((2, nz)), dma((nz,)), dma, dma,
         dma((2, nz, chunks)), dma((nz, chunks)), dma((2, nz)), dma((2, nz)), dma((nz,)), dma((nz,)),
-        dma((2, nz)), dma((2, nz)), dma((nz,)), dma((nz,)), dma((nz, sums)), dma((nz, sums)), dma((nz, sums)), dma, dma,
+        dma((2, nz)), dma((2, nz)), dma((nz,)), dma((nz,)), dma, dma, dma((sums,)), dma((sums,)), dma((sums,)), dma((sums,)),
+        dma((nz, sums)), dma((nz, sums)), dma((nz, sums)), dma, dma,
     ]
     in_vmem, in_hbm = pl.BlockSpec(memory_space=pltpu.VMEM), pl.BlockSpec(memory_space=pl.ANY)
     return pl.pallas_call(

time: 77.1 us -> 74 us (0.960)
  Pallas kernels: 75.2 us -> 72.1 us
    pallas_call x1, Pallas kernels: 75.2 us -> 72.1 us  [gather_local(): pl.pallas_call(functools.partial(moe_kernel, nz, nx, cap), out_shape=jax....]
where the time goes in v4:
time: 74 us; the launch traced here: 73.8 us
  Pallas kernels  72.1 us (97%)
  local copies, waits for them, and re-layouts  1.75 us (2%)
    pallas_call x1, Pallas kernels, gather_local(): pl.pallas_call(functools.partial(moe_kernel, nz, nx, cap), out_shape=jax....  72.1 us
    unnamed x1, local copies, waits for them, and re-layouts  1.75 us

profile of v4, /device:TPU:1, one launch (start us, length us, event | category | flops | bytes accessed | tf_op | source)
XLA Modules:
  0.0 73.8 jit_solution(8919286542362961001)
XLA Ops:
  0.0 72.1 %shard_map.91 = bf16[720,256]{1,0:T(8,128)(2,1)} custom-call(bf16[1440,256]{1,0:T(8,128)(2,1)} %bitcast.5, s32[4,256]{1,0:T(4,128)} %bitcast.6, f32[4,256]{1,0:T(4,128)} %bitcast.7, bf16[1,1440,720]{2,1,0:T(8,128)(2,1)} %wg_ref.1, bf16[1,1440,720]{2,1,0:T(8,128)(2,1)} %wu_ref.1, bf16[1,720,1440]{2,1,0:T(8,128)(2,1)} %wd_ref.1, bf16[1440,720]{1,0:T(8,128)(2,1)} %sg_ref.1, ...), custom_call_target="tpu_custom_call" | custom-call | tf_op jit(solution)/shard_map/pallas_call | solution.py:503
  72.1 1.7 %copy.11 = bf16[256,720]{0,1:T(8,128)(2,1)} copy(bf16[256,720]{0,1:T(8,128)(2,1)} %bitcast.4) | data formatting | bytes 737280

commit v5 on v4

--- a/solution.py
+++ b/solution.py
@@ -481,7 +481,7 @@
     cap = most_named(tok_count, top, n)
     ch = cap // 2
     chunks = next(c for c in (3, 2, 1) if half % (16 * c) == 0)
-    sums = chunks
+    sums = next(c for c in (5, 3, 2, 1) if half % (16 * c) == 0)
     bf, f32 = jnp.bfloat16, jnp.float32
     vm, dma = pltpu.VMEM, pltpu.SemaphoreType.DMA
     scratch = [

time: 74 us -> 73.4 us (level)
  no operation moved by 1% of the time
where the time goes in v5:
time: 73.4 us; the launch traced here: 73.2 us
  Pallas kernels  71.4 us (97%)
  local copies, waits for them, and re-layouts  1.75 us (2%)
    pallas_call x1, Pallas kernels, gather_local(): pl.pallas_call(functools.partial(moe_kernel, nz, nx, cap), out_shape=jax....  71.4 us
    unnamed x1, local copies, waits for them, and re-layouts  1.75 us

profile of v5, /device:TPU:1, one launch (start us, length us, event | category | flops | bytes accessed | tf_op | source)
XLA Modules:
  0.0 73.2 jit_solution(15571996486127937326)
XLA Ops:
  0.0 71.4 %shard_map.91 = bf16[720,256]{1,0:T(8,128)(2,1)} custom-call(bf16[1440,256]{1,0:T(8,128)(2,1)} %bitcast.5, s32[4,256]{1,0:T(4,128)} %bitcast.6, f32[4,256]{1,0:T(4,128)} %bitcast.7, bf16[1,1440,720]{2,1,0:T(8,128)(2,1)} %wg_ref.1, bf16[1,1440,720]{2,1,0:T(8,128)(2,1)} %wu_ref.1, bf16[1,720,1440]{2,1,0:T(8,128)(2,1)} %wd_ref.1, bf16[1440,720]{1,0:T(8,128)(2,1)} %sg_ref.1, ...), custom_call_target="tpu_custom_call" | custom-call | tf_op jit(solution)/shard_map/pallas_call | solution.py:503
  71.4 1.7 %copy.11 = bf16[256,720]{0,1:T(8,128)(2,1)} copy(bf16[256,720]{0,1:T(8,128)(2,1)} %bitcast.4) | data formatting | bytes 737280
